TPU v7x, 32 devices: a whole 2x2x4 slice. The times are simulated.
32 devices in a mesh: dp: 8 (over y, x, core), mp: 4 (over z).
Axes of the slice: x: 2, y: 2, z: 4, core: 2. Of those that a mesh axis runs over, the one named last changes fastest.
Arguments:
- saved_query: bfloat16 [2048, 4096], P('dp', 'mp'), may hold values from -80 to 80
- saved_key: bfloat16 [2048, 1024], P('dp', 'mp'), may hold values from -16 to 16
- saved_value: bfloat16 [2048, 1024], P('dp', 'mp'), may hold values from -6 to 6
- grad_output: bfloat16 [2048, 4096], P('dp', 'mp'), may hold values from -24 to 24
- unit_server: int32 [64], P('dp'), may hold values from 0 to 7, as said below
- unit_place: int32 [64], P('dp'), may hold values from 0 to 7, as said below
- doc_length: int32 [8], P('dp'), may hold values from 1 to 256
- query_weight: bfloat16 [4096, 4096], P(None, 'mp'), may hold values from -0.078125 to 0.078125
- key_weight: bfloat16 [4096, 1024], P(None, 'mp'), may hold values from -0.078125 to 0.078125
- value_weight: bfloat16 [4096, 1024], P(None, 'mp'), may hold values from -0.078125 to 0.078125
Outputs:
- grad_input: float32 [2048, 4096], P('dp', 'mp')
Inputs may be any that keep to these rules, and one draw needn't show every extreme that they name: `unit_server`: each server receives exactly 8 units, exactly one from the units of each device along dp; the units of one document block come from 8 different devices. The pairs (unit_server, unit_place) are all different, so each server's places 0 to 7 are each taken once.
All inputs are finite; a program needn't handle non-finite values.
Results may differ from a plain program's by a relative error of at most 0.011.
Values may be sent and summed in bfloat16 or wider, within the bound.
No kernel may reach another device: no remote copies, remote signals or barrier semaphores. Data moves between devices by JAX's collectives and lax.ppermute only.
A program may use at most 128 MiB of HBM per device.

v0:
```python
import math

import jax
import jax.numpy as jnp
from jax import lax
from jax.sharding import PartitionSpec as P

HEAD = 128
DOC_UNITS = 8


def tile_backward(query_rows, key_rows, value_rows, grad_rows, length, kv_heads):
    query_count = query_rows.shape[0]
    key_count = key_rows.shape[0]
    group_size = query_rows.shape[1] // (kv_heads * HEAD)
    score_scale = 1.0 / math.sqrt(HEAD)
    queries = query_rows.reshape(query_count, kv_heads, group_size, HEAD)
    keys = key_rows.reshape(key_count, kv_heads, HEAD)
    values = value_rows.reshape(key_count, kv_heads, HEAD)
    query_index = jnp.arange(query_count, dtype=jnp.int32)
    key_index = jnp.arange(key_count, dtype=jnp.int32)
    live_rows = (query_index < length).astype(grad_rows.dtype)
    masked = (grad_rows * live_rows[:, None]).reshape(query_count, kv_heads, group_size, HEAD)
    allowed = (key_index[None, :] <= query_index[:, None]) & (key_index[None, :] < length)
    scores = (
        jnp.einsum("ikgd,jkd->kgij", queries, keys, preferred_element_type=jnp.float32)
        * score_scale
    )
    scores = jnp.where(allowed, scores, -1e30)
    row_peak = jnp.max(scores, axis=-1, keepdims=True)
    expanded = jnp.where(allowed, jnp.exp(scores - row_peak), 0.0)
    attention = expanded / jnp.sum(expanded, axis=-1, keepdims=True)
    attention_low = attention.astype(jnp.bfloat16)
    attended = jnp.einsum(
        "kgij,jkd->ikgd", attention_low, values, preferred_element_type=jnp.float32
    )
    row_delta = jnp.sum(masked * attended, axis=-1)
    prob_grad = jnp.einsum("ikgd,jkd->kgij", masked, values, preferred_element_type=jnp.float32)
    score_grad = attention * (prob_grad - jnp.transpose(row_delta, (1, 2, 0))[..., None])
    score_low = score_grad.astype(jnp.bfloat16)
    query_grad = (
        jnp.einsum("kgij,jkd->ikgd", score_low, keys, preferred_element_type=jnp.float32)
        * score_scale
    )
    key_grad = (
        jnp.einsum("kgij,ikgd->jkd", score_low, queries, preferred_element_type=jnp.float32)
        * score_scale
    )
    value_grad = jnp.einsum(
        "kgij,ikgd->jkd", attention_low, masked, preferred_element_type=jnp.float32
    )
    return (
        query_grad.reshape(query_count, -1),
        key_grad.reshape(key_count, -1),
        value_grad.reshape(key_count, -1),
    )


def project(grads, query_weight, key_weight, value_weight):
    numbers = (((1,), (1,)), ((), ()))
    summed = lax.dot_general(grads[0], query_weight, numbers, preferred_element_type=jnp.float32)
    summed = summed + lax.dot_general(
        grads[1], key_weight, numbers, preferred_element_type=jnp.float32
    )
    return summed + lax.dot_general(
        grads[2], value_weight, numbers, preferred_element_type=jnp.float32
    )


def local(
    saved_query,
    saved_key,
    saved_value,
    grad_output,
    unit_server,
    unit_place,
    doc_length,
    query_weight,
    key_weight,
    value_weight,
):
    server_count = lax.axis_size("dp")
    unit_count = unit_server.shape[0]
    unit_rows = saved_query.shape[0] // unit_count
    block_rows = DOC_UNITS * unit_rows
    doc_count = unit_count // DOC_UNITS
    kv_heads = saved_key.shape[1] // HEAD

    def outgoing(tensor):
        pieces = tensor.reshape(unit_count, unit_rows, tensor.shape[1])
        return (
            jnp.zeros((server_count, unit_rows, tensor.shape[1]), tensor.dtype)
            .at[unit_server]
            .set(pieces)
        )

    places = jnp.full((server_count,), -1, jnp.int32).at[unit_server].set(unit_place)
    arrived = (
        lax.all_to_all(outgoing(saved_query), "dp", split_axis=0, concat_axis=0, tiled=True),
        lax.all_to_all(outgoing(saved_key), "dp", split_axis=0, concat_axis=0, tiled=True),
        lax.all_to_all(outgoing(saved_value), "dp", split_axis=0, concat_axis=0, tiled=True),
        lax.all_to_all(outgoing(grad_output), "dp", split_axis=0, concat_axis=0, tiled=True),
        lax.all_to_all(places, "dp", split_axis=0, concat_axis=0, tiled=True),
    )
    matches = arrived[4][None, :] == jnp.arange(unit_count, dtype=jnp.int32)[:, None]
    source = jnp.sum(
        jnp.where(matches, jnp.arange(server_count, dtype=jnp.int32)[None, :], 0), axis=1
    )

    def assemble(tensor):
        return tensor[source].reshape(doc_count, block_rows, tensor.shape[2])

    doc_query = assemble(arrived[0])
    doc_key = assemble(arrived[1])
    doc_value = assemble(arrived[2])
    doc_grad = assemble(arrived[3])
    query_parts = []
    key_parts = []
    value_parts = []
    for doc_index in range(doc_count):
        length = doc_length[doc_index]
        query_total, key_total, value_total = tile_backward(
            doc_query[doc_index],
            doc_key[doc_index],
            doc_value[doc_index],
            doc_grad[doc_index],
            length,
            kv_heads,
        )
        query_parts.append(query_total.astype(jnp.bfloat16))
        key_parts.append(key_total.astype(jnp.bfloat16))
        value_parts.append(value_total.astype(jnp.bfloat16))
    query_units = jnp.concatenate(query_parts, axis=0)
    key_units = jnp.concatenate(key_parts, axis=0)
    value_units = jnp.concatenate(value_parts, axis=0)
    partial_value = project(
        (query_units, key_units, value_units), query_weight, key_weight, value_weight
    )
    columns = lax.psum_scatter(partial_value, "mp", scatter_dimension=1, tiled=True)
    pieces = columns.reshape(unit_count, unit_rows, columns.shape[-1])
    back = lax.all_to_all(
        jnp.zeros((server_count, unit_rows, columns.shape[-1]), columns.dtype)
        .at[source]
        .set(pieces),
        "dp",
        split_axis=0,
        concat_axis=0,
        tiled=True,
    )
    return back[unit_server].reshape(unit_count * unit_rows, back.shape[2])


def solution(mesh):
    placed = (
        P("dp", "mp"),
        P("dp", "mp"),
        P("dp", "mp"),
        P("dp", "mp"),
        P("dp"),
        P("dp"),
        P("dp"),
        P(None, "mp"),
        P(None, "mp"),
        P(None, "mp"),
    )
    return jax.shard_map(
        local, mesh=mesh, in_specs=placed, out_specs=P("dp", "mp"), check_vma=False
    )
```

profile of v0, /device:TPU:0, one launch (start us, length us, event | category | flops | bytes accessed | tf_op | source)
XLA Modules:
  0.0 191.8 jit_solution(12859446028088509334)
XLA Ops:
  6.5 0.8 compare_select_fusion.1
  7.4 0.7 scatter_custom_fusion
  8.1 0.7 copy.57
  8.8 5.2 %all-to-all-start = ((s32[8,1,1]{2,1,0:T(1,128)}), s32[8,1,1]{2,1,0:T(1,128)S(1)}, u32[]{:S(2)}, u32[]{:S(2)}) async-start(s32[8,1,1]{2,1,0:T(1,128)} %copy.57), calls=%async_computation | async-start | bytes 8192 | tf_op jit(solution)/shard_map/all_to_all | solution.py:103
  14.0 0.7 broadcast.60.clone
  14.6 2.3 %scatter_fusion = bf16[8,32,256]{2,1,0:T(8,128)(2,1)} fusion(bf16[8,32,256]{2,1,0:T(8,128)(2,1)} %broadcast.60.clone, s32[8]{0:T(128)S(1)} %compare_select_fusion.1, bf16[8,32,256]{2,1,0:T(8,128)(2,1)} %bitcast.88), kind=kCustom, calls=%fused_computation.6 | custom fusion | bytes 393248 | tf_op jit(solution)/shard_map/scatter | solution.py:94
  16.9 1.7 all-to-all-done
  18.6 3.4 %all-to-all-start.1 = ((bf16[8,32,256]{2,1,0:T(8,128)(2,1)}), bf16[8,32,256]{2,1,0:T(8,128)(2,1)S(1)}, u32[]{:S(2)}, u32[]{:S(2)}) async-start(bf16[8,32,256]{2,1,0:T(8,128)(2,1)} %scatter_fusion), calls=%async_computation.1 | async-start | bytes 262144 | tf_op jit(solution)/shard_map/all_to_all | solution.py:100
  22.0 0.6 broadcast.60.clone.1
  22.7 2.3 %scatter_fusion.2 = bf16[8,32,256]{2,1,0:T(8,128)(2,1)} fusion(bf16[8,32,256]{2,1,0:T(8,128)(2,1)} %broadcast.60.clone.1, s32[8]{0:T(128)S(1)} %compare_select_fusion.1, bf16[8,32,256]{2,1,0:T(8,128)(2,1)} %bitcast.89), kind=kCustom, calls=%fused_computation.8 | custom fusion | bytes 393248 | tf_op jit(solution)/shard_map/scatter | solution.py:94
  24.9 2.5 %all-to-all-done.1 = bf16[8,32,256]{2,1,0:T(8,128)(2,1)S(1)} async-done(((bf16[8,32,256]{2,1,0:T(8,128)(2,1)}), bf16[8,32,256]{2,1,0:T(8,128)(2,1)S(1)}, u32[]{:S(2)}, u32[]{:S(2)}) %all-to-all-start.1) | async-done | bytes 131104 | tf_op jit(solution)/shard_map/all_to_all | solution.py:100
  27.5 3.4 %all-to-all-start.3 = ((bf16[8,32,256]{2,1,0:T(8,128)(2,1)}), bf16[8,32,256]{2,1,0:T(8,128)(2,1)S(1)}, u32[]{:S(2)}, u32[]{:S(2)}) async-start(bf16[8,32,256]{2,1,0:T(8,128)(2,1)} %scatter_fusion.2), calls=%async_computation.3 | async-start | bytes 262144 | tf_op jit(solution)/shard_map/all_to_all | solution.py:101
  30.8 0.9 broadcast.61.clone
  31.7 2.5 %scatter_fusion.1 = bf16[8,32,1024]{2,1,0:T(8,128)(2,1)} fusion(bf16[8,32,1024]{2,1,0:T(8,128)(2,1)} %broadcast.61.clone, s32[8]{0:T(128)S(1)} %compare_select_fusion.1, bf16[8,32,1024]{2,1,0:T(8,128)(2,1)S(1)} %bitcast.82), kind=kCustom, calls=%fused_computation.7 | custom fusion | bytes 1572896 | tf_op jit(solution)/shard_map/scatter | solution.py:94
  34.1 2.1 %all-to-all-done.3 = bf16[8,32,256]{2,1,0:T(8,128)(2,1)S(1)} async-done(((bf16[8,32,256]{2,1,0:T(8,128)(2,1)}), bf16[8,32,256]{2,1,0:T(8,128)(2,1)S(1)}, u32[]{:S(2)}, u32[]{:S(2)}) %all-to-all-start.3) | async-done | bytes 131104 | tf_op jit(solution)/shard_map/all_to_all | solution.py:101
  36.3 3.5 %all-to-all-start.2 = ((bf16[8,32,1024]{2,1,0:T(8,128)(2,1)}), bf16[8,32,1024]{2,1,0:T(8,128)(2,1)S(1)}, u32[]{:S(2)}, u32[]{:S(2)}) async-start(bf16[8,32,1024]{2,1,0:T(8,128)(2,1)} %scatter_fusion.1), calls=%async_computation.2 | async-start | bytes 1048576 | tf_op jit(solution)/shard_map/all_to_all | solution.py:99
  40.4 0.9 broadcast.61.clone.1
  41.3 2.5 %scatter_fusion.3 = bf16[8,32,1024]{2,1,0:T(8,128)(2,1)} fusion(bf16[8,32,1024]{2,1,0:T(8,128)(2,1)} %broadcast.61.clone.1, s32[8]{0:T(128)S(1)} %compare_select_fusion.1, bf16[8,32,1024]{2,1,0:T(8,128)(2,1)S(1)} %bitcast.83), kind=kCustom, calls=%fused_computation.9 | custom fusion | bytes 1572896 | tf_op jit(solution)/shard_map/scatter | solution.py:94
  43.7 0.7 fusion.18
  44.5 5.0 %all-to-all-done.2 = bf16[8,32,1024]{2,1,0:T(8,128)(2,1)S(1)} async-done(((bf16[8,32,1024]{2,1,0:T(8,128)(2,1)}), bf16[8,32,1024]{2,1,0:T(8,128)(2,1)S(1)}, u32[]{:S(2)}, u32[]{:S(2)}) %all-to-all-start.2) | async-done | bytes 524320 | tf_op jit(solution)/shard_map/all_to_all | solution.py:99
  49.4 3.5 %all-to-all-start.4 = ((bf16[8,32,1024]{2,1,0:T(8,128)(2,1)}), bf16[8,32,1024]{2,1,0:T(8,128)(2,1)S(1)}, u32[]{:S(2)}, u32[]{:S(2)}) async-start(bf16[8,32,1024]{2,1,0:T(8,128)(2,1)} %scatter_fusion.3), calls=%async_computation.4 | async-start | bytes 1048576 | tf_op jit(solution)/shard_map/all_to_all | solution.py:102
  53.4 0.6 gather_fusion
  54.1 0.6 gather_fusion.2
  54.8 1.4 gather_fusion.1
  56.2 2.2 %reshape_squeeze_reshape.10 = bf16[256,2,4,128]{3,2,1,0:T(4,128)(2,1)} reshape(bf16[8,32,1024]{2,1,0:T(8,128)(2,1)} %gather_fusion.1) | data formatting | bytes 1048576 | tf_op jit(solution)/shard_map/reshape;squeeze;reshape | solution.py:17
  58.4 1.4 copy.67
  59.7 2.8 %all-to-all-done.4 = bf16[8,32,1024]{2,1,0:T(8,128)(2,1)S(1)} async-done(((bf16[8,32,1024]{2,1,0:T(8,128)(2,1)}), bf16[8,32,1024]{2,1,0:T(8,128)(2,1)S(1)}, u32[]{:S(2)}, u32[]{:S(2)}) %all-to-all-start.4) | async-done | bytes 524320 | tf_op jit(solution)/shard_map/all_to_all | solution.py:102
  62.6 1.4 gather_fusion.3
  63.9 1.4 squeeze_reshape.3
  65.4 1.1 copy.60
  66.5 2.3 %fusion.27 = (f32[2,4,256]{2,1,0:T(4,128)S(1)}, f32[2,4,256,256]{2,3,1,0:T(8,128)}) fusion(pred[256,256]{0,1:T(8,128)(4,1)S(1)} %copy-done.6, bf16[256,2,128,1]{0,2,3,1:T(8,128)(2,1)S(1)} %copy.75, bf16[256,2,4,128]{0,3,2,1:T(8,128)(2,1)S(1)} %copy.67), kind=kOutput, calls=%fused_computation.55 | convolution fusion | flops 136839424 | bytes 2826240 | tf_op jit(solution)/shard_map/sub | solution.py:31
  68.8 1.8 fusion.13
  70.7 0.5 fusion.8
  71.1 0.3 fusion.6
  71.5 0.8 copy-done.1
  72.2 0.5 fusion.2
  72.7 0.5 fusion.9
  73.2 0.3 fusion.5
  73.5 5.8 %fusion.28 = f32[256,4096]{1,0:T(8,128)S(1)} fusion(bf16[256,1024]{0,1:T(8,128)(2,1)S(1)} %bitcast.84, bf16[4096,1024]{1,0:T(8,128)(2,1)} %param.17), kind=kOutput, calls=%fused_computation.56 | convolution fusion | flops 2147483648 | bytes 13107200 | tf_op jit(solution)/shard_map/dot_general | solution.py:61
  79.4 0.8 convolution_add_fusion.1
  80.1 0.8 copy-done.2
  80.9 2.7 %convolution_add_fusion = f32[256,4096]{1,0:T(8,128)} fusion(f32[256,4096]{1,0:T(8,128)S(1)} %convolution_add_fusion.1, bf16[256,256]{0,1:T(8,128)(2,1)S(1)} %bitcast.90, bf16[4096,256]{1,0:T(8,128)(2,1)S(1)} %copy-done.2), kind=kOutput, calls=%fused_computation.12 | convolution fusion | flops 537919488 | bytes 10616832 | tf_op jit(solution)/shard_map/dot_general | solution.py:65
  83.7 76.3 %reduce-scatter.2.cloned.1.call-done = f32[256,1024]{1,0:T(8,128)} async-done(((f32[256,4096]{1,0:T(8,128)}), f32[256,1024]{1,0:T(8,128)}) %reduce-scatter.2.cloned.1.call-update) | async-done | bytes 1048592 | tf_op jit(solution)/shard_map/reduce_scatter | solution.py:139
  160.0 1.1 broadcast_in_dim.26
  161.1 3.2 %scatter_fusion.4 = f32[8,32,1024]{2,1,0:T(8,128)} fusion(f32[8,32,1024]{2,1,0:T(8,128)} %broadcast_in_dim.26, s32[8]{0:T(128)S(1)} %fusion.21, f32[8,32,1024]{2,1,0:T(8,128)} %bitcast.81), kind=kCustom, calls=%fused_computation.10 | custom fusion | bytes 3145760 | tf_op jit(solution)/shard_map/scatter | solution.py:144
  164.3 3.7 %all-to-all-start.5 = ((f32[8,32,1024]{2,1,0:T(8,128)}), f32[8,32,1024]{2,1,0:T(8,128)S(1)}, u32[]{:S(2)}, u32[]{:S(2)}) async-start(f32[8,32,1024]{2,1,0:T(8,128)} %scatter_fusion.4), calls=%async_computation.6 | async-start | bytes 2097152 | tf_op jit(solution)/shard_map/all_to_all | solution.py:141
  168.0 15.4 %all-to-all-done.5 = f32[8,32,1024]{2,1,0:T(8,128)S(1)} async-done(((f32[8,32,1024]{2,1,0:T(8,128)}), f32[8,32,1024]{2,1,0:T(8,128)S(1)}, u32[]{:S(2)}, u32[]{:S(2)}) %all-to-all-start.5) | async-done | bytes 1048608 | tf_op jit(solution)/shard_map/all_to_all | solution.py:141
  183.4 1.6 gather_fusion.4
  (25 shorter events, 0.8 us)
Async XLA Ops:
  6.5 72.8 %copy-start = (bf16[4096,256]{1,0:T(8,128)(2,1)S(1)}, bf16[4096,256]{1,0:T(8,128)(2,1)}, u32[]{:S(2)}) copy-start(bf16[4096,256]{1,0:T(8,128)(2,1)} %param.18) | copy-start | bytes 6291460
  6.5 25.2 %copy-start.3 = (bf16[256,1024]{1,0:T(8,128)(2,1)S(1)}, bf16[256,1024]{1,0:T(8,128)(2,1)}, u32[]{:S(2)}) copy-start(bf16[256,1024]{1,0:T(8,128)(2,1)} %param.10) | copy-start | bytes 1572868
  8.8 9.9 %all-to-all-start = ((s32[8,1,1]{2,1,0:T(1,128)}), s32[8,1,1]{2,1,0:T(1,128)S(1)}, u32[]{:S(2)}, u32[]{:S(2)}) async-start(s32[8,1,1]{2,1,0:T(1,128)} %copy.57), calls=%async_computation | async-start | bytes 8192 | tf_op jit(solution)/shard_map/all_to_all | solution.py:103
  18.6 8.8 %all-to-all-start.1 = ((bf16[8,32,256]{2,1,0:T(8,128)(2,1)}), bf16[8,32,256]{2,1,0:T(8,128)(2,1)S(1)}, u32[]{:S(2)}, u32[]{:S(2)}) async-start(bf16[8,32,256]{2,1,0:T(8,128)(2,1)} %scatter_fusion), calls=%async_computation.1 | async-start | bytes 262144 | tf_op jit(solution)/shard_map/all_to_all | solution.py:100
  22.7 18.6 %copy-start.4 = (bf16[256,1024]{1,0:T(8,128)(2,1)S(1)}, bf16[256,1024]{1,0:T(8,128)(2,1)}, u32[]{:S(2)}) copy-start(bf16[256,1024]{1,0:T(8,128)(2,1)} %param.13) | copy-start | bytes 1572868
  27.5 8.8 %all-to-all-start.3 = ((bf16[8,32,256]{2,1,0:T(8,128)(2,1)}), bf16[8,32,256]{2,1,0:T(8,128)(2,1)S(1)}, u32[]{:S(2)}, u32[]{:S(2)}) async-start(bf16[8,32,256]{2,1,0:T(8,128)(2,1)} %scatter_fusion.2), calls=%async_computation.3 | async-start | bytes 262144 | tf_op jit(solution)/shard_map/all_to_all | solution.py:101
  36.3 13.2 %all-to-all-start.2 = ((bf16[8,32,1024]{2,1,0:T(8,128)(2,1)}), bf16[8,32,1024]{2,1,0:T(8,128)(2,1)S(1)}, u32[]{:S(2)}, u32[]{:S(2)}) async-start(bf16[8,32,1024]{2,1,0:T(8,128)(2,1)} %scatter_fusion.1), calls=%async_computation.2 | async-start | bytes 1048576 | tf_op jit(solution)/shard_map/all_to_all | solution.py:99
  49.4 13.1 %all-to-all-start.4 = ((bf16[8,32,1024]{2,1,0:T(8,128)(2,1)}), bf16[8,32,1024]{2,1,0:T(8,128)(2,1)S(1)}, u32[]{:S(2)}, u32[]{:S(2)}) async-start(bf16[8,32,1024]{2,1,0:T(8,128)(2,1)} %scatter_fusion.3), calls=%async_computation.4 | async-start | bytes 1048576 | tf_op jit(solution)/shard_map/all_to_all | solution.py:102
  52.9 107.1 %reduce-scatter.2.cloned.1.call-start = ((), (), s32[]{:S(2)}) async-start(), calls=%async_computation.7 | async-start | bytes 5242880 | tf_op jit(solution)/shard_map/reduce_scatter | solution.py:139
  58.4 8.1 %copy-start.6 = (pred[256,256]{0,1:T(8,128)(4,1)S(1)}, pred[256,256]{0,1:T(8,128)(4,1)}, u32[]{:S(2)}) copy-start(pred[256,256]{0,1:T(8,128)(4,1)} %fusion.18) | copy-start | bytes 196612
  68.8 1.8 copy-start.5
  70.6 1.6 copy-start.1
  79.3 1.6 copy-start.2
  164.3 19.0 %all-to-all-start.5 = ((f32[8,32,1024]{2,1,0:T(8,128)}), f32[8,32,1024]{2,1,0:T(8,128)S(1)}, u32[]{:S(2)}, u32[]{:S(2)}) async-start(f32[8,32,1024]{2,1,0:T(8,128)} %scatter_fusion.4), calls=%async_computation.6 | async-start | bytes 2097152 | tf_op jit(solution)/shard_map/all_to_all | solution.py:141
Sparse Core Ops, SparseCore 0:
  83.8 76.1 reduce-scatter.1
where the time goes:
time: 193 us; the launch traced here: 192 us
  waiting for transfers between devices  106 us (55%)
  local copies, waits for them, and re-layouts  31.6 us (16%)
  starting transfers between devices  22.6 us (12%)
  between operations  14.3 us (7%)
  matrix products  13.7 us (7%)
  other arithmetic  3.74 us (2%)
    reduce_scatter x1, waiting for transfers between devices, local(): lax.psum_scatter(partial_value, 'mp', scatter_dimension=1, tiled=True)  76.3 us
    all_to_all x1, waiting for transfers between devices, local(): lax.all_to_all(jnp.zeros((server_count, unit_rows, columns.shape[-1]), co...  15.4 us
    scatter x4, local copies, waits for them, and re-layouts, outgoing(): return jnp.zeros((server_count, unit_rows, tensor.shape[1]), tensor.dtype...  9.46 us
    dot_general x1, matrix products, project(): lax.dot_general(grads[0], query_weight, numbers, preferred_element_type=j...  5.77 us
    all_to_all x1, starting transfers between devices, local(): lax.all_to_all(places, 'dp', split_axis=0, concat_axis=0, tiled=True)  5.2 us
    all_to_all x1, waiting for transfers between devices, local(): lax.all_to_all(outgoing(saved_query), 'dp', split_axis=0, concat_axis=0,...  4.95 us
  transfers between devices with their start and end apart: 7, of which 7 were waited for; matrix products, arithmetic and copies ran while one was open for 10% of the time, Pallas kernels for 0%

commit v1 on v0

v1 whole, which is shorter than its diff:
```python
import functools
import math

import jax
import jax.numpy as jnp
from jax import lax
from jax.experimental import pallas as pl
from jax.experimental.pallas import tpu as pltpu
from jax.sharding import PartitionSpec as P

HEAD = 128
DOC_UNITS = 8
LANES = 128


def pack_kernel(server_ref, place_ref, q_ref, k_ref, v_ref, g_ref, out_ref):
    units = out_ref.shape[0]
    unit_rows = out_ref.shape[1]
    for u in range(units):
        slot = server_ref[u]
        rows = pl.ds(u * unit_rows, unit_rows)
        at = 0
        for ref in (q_ref, k_ref, v_ref, g_ref):
            width = ref.shape[1]
            out_ref[slot, :, at : at + width] = ref[rows, :]
            at += width
        place = jnp.full((unit_rows, LANES), place_ref[u], jnp.int32)
        out_ref[slot, :, at : at + LANES] = place.astype(jnp.float32).astype(out_ref.dtype)


def pack(unit_server, unit_place, q, k, v, g):
    units = unit_server.shape[0]
    width = q.shape[1] + k.shape[1] + v.shape[1] + g.shape[1] + LANES
    smem = pl.BlockSpec(memory_space=pltpu.SMEM)
    vmem = pl.BlockSpec(memory_space=pltpu.VMEM)
    return pl.pallas_call(
        pack_kernel,
        out_shape=jax.ShapeDtypeStruct((units, q.shape[0] // units, width), q.dtype),
        in_specs=[smem, smem, vmem, vmem, vmem, vmem],
        out_specs=vmem,
        name="pack",
    )(unit_server, unit_place, q, k, v, g)


NT = (((1,), (1,)), ((), ()))
TN = (((0,), (0,)), ((), ()))


def dot(a, b, numbers):
    return lax.dot_general(a, b, numbers, preferred_element_type=jnp.float32)


def server_kernel(
    kv_heads,
    tile,
    length_ref,
    arrived_ref,
    qw_hbm,
    kw_hbm,
    vw_hbm,
    out_hbm,
    qw,
    kw,
    vw,
    grads,
    partial,
    in_sems,
    out_sems,
):
    doc_count = length_ref.shape[0]
    slots, unit_rows, _ = arrived_ref.shape
    block_rows = slots * unit_rows // doc_count
    doc_slots = slots // doc_count
    parts = out_hbm.shape[1]
    part_width = out_hbm.shape[3]
    q_width = qw.shape[1]
    kv_width = kw.shape[1]
    group = q_width // kv_width
    scale = 1.0 / math.sqrt(HEAD)

    def weight_copies(part):
        rows = pl.ds(part * part_width, part_width)
        return [
            pltpu.make_async_copy(hbm.at[rows], vmem.at[rows], in_sems.at[part, n])
            for n, (hbm, vmem) in enumerate(((qw_hbm, qw), (kw_hbm, kw), (vw_hbm, vw)))
        ]

    for part in range(parts):
        for copy in weight_copies(part):
            copy.start()

    for doc in range(doc_count):
        here = pl.ds(doc * doc_slots, doc_slots)
        rows = pl.ds(doc * block_rows, block_rows)
        length = length_ref[doc].astype(jnp.float32)

        def load(at, width):
            return arrived_ref[here, :, at : at + width].reshape(block_rows, width)

        at_place = 2 * (q_width + kv_width)
        place = load(at_place, LANES).astype(jnp.float32)
        row = lax.broadcasted_iota(jnp.int32, (block_rows, LANES), 0).astype(jnp.float32)
        slot = jnp.floor(row * (1.0 / unit_rows))
        place = place - DOC_UNITS * jnp.floor(place * (1.0 / DOC_UNITS))
        position = place * unit_rows + (row - slot * unit_rows)
        query_at = position[:, :1]
        key_at = jnp.transpose(position)[:1, :]
        allowed = (key_at <= query_at) & (key_at < length)
        live = query_at < length
        for kv in range(kv_heads):
            keys = load(q_width + kv * HEAD, HEAD)
            values = load(q_width + kv_width + kv * HEAD, HEAD)
            key_grad = None
            value_grad = None
            for h in range(kv * group, (kv + 1) * group):
                queries = load(h * HEAD, HEAD)
                outer = load(q_width + 2 * kv_width + h * HEAD, HEAD)
                masked = jnp.where(live, outer.astype(jnp.float32), 0.0).astype(jnp.bfloat16)
                scores = dot(queries, keys, NT) * scale
                scores = jnp.where(allowed, scores, -1e30)
                peak = jnp.max(scores, axis=1, keepdims=True)
                expanded = jnp.where(allowed, jnp.exp(scores - peak), 0.0)
                probs = expanded * (1.0 / jnp.sum(expanded, axis=1, keepdims=True))
                probs_low = probs.astype(jnp.bfloat16)
                prob_grad = dot(masked, values, NT)
                delta = jnp.sum(probs_low.astype(jnp.float32) * prob_grad, axis=1, keepdims=True)
                score_low = (probs * (prob_grad - delta)).astype(jnp.bfloat16)
                query_grad = dot(score_low, keys, (((1,), (0,)), ((), ()))) * scale
                grads[rows, h * HEAD : (h + 1) * HEAD] = query_grad.astype(jnp.bfloat16)
                dk = dot(score_low, queries, TN)
                dv = dot(probs_low, masked, TN)
                key_grad = dk if key_grad is None else key_grad + dk
                value_grad = dv if value_grad is None else value_grad + dv
            at = q_width + kv * HEAD
            grads[rows, at : at + HEAD] = (key_grad * scale).astype(jnp.bfloat16)
            at = q_width + kv_width + kv * HEAD
            grads[rows, at : at + HEAD] = value_grad.astype(jnp.bfloat16)

    def out_copy(part):
        return pltpu.make_async_copy(
            partial.at[part], out_hbm.at[:, part], out_sems.at[part]
        )

    for part in range(parts):
        for copy in weight_copies(part):
            copy.wait()
        for at in range(0, part_width, tile):
            columns = pl.ds(part * part_width + at, tile)
            total = dot(grads[:, :q_width], qw[columns, :], NT)
            total = total + dot(grads[:, q_width : q_width + kv_width], kw[columns, :], NT)
            total = total + dot(grads[:, q_width + kv_width :], vw[columns, :], NT)
            partial[part, :, :, at : at + tile] = total.astype(jnp.bfloat16).reshape(
                slots, unit_rows, tile
            )
        out_copy(part).start()
    for part in range(parts):
        out_copy(part).wait()


def serve(doc_length, arrived, qw, kw, vw, parts):
    slots, unit_rows, _ = arrived.shape
    width = qw.shape[0]
    part_width = width // parts
    kv_heads = kw.shape[1] // HEAD
    rows = slots * unit_rows
    hbm = pl.BlockSpec(memory_space=pl.ANY)
    bf16 = jnp.bfloat16
    return pl.pallas_call(
        functools.partial(server_kernel, kv_heads, min(256, part_width)),
        out_shape=jax.ShapeDtypeStruct((slots, parts, unit_rows, part_width), bf16),
        in_specs=[
            pl.BlockSpec(memory_space=pltpu.SMEM),
            pl.BlockSpec(memory_space=pltpu.VMEM),
            hbm,
            hbm,
            hbm,
        ],
        out_specs=hbm,
        scratch_shapes=[
            pltpu.VMEM(qw.shape, bf16),
            pltpu.VMEM(kw.shape, bf16),
            pltpu.VMEM(vw.shape, bf16),
            pltpu.VMEM((rows, qw.shape[1] + 2 * kw.shape[1]), bf16),
            pltpu.VMEM((parts, slots, unit_rows, part_width), bf16),
            pltpu.SemaphoreType.DMA((parts, 3)),
            pltpu.SemaphoreType.DMA((parts,)),
        ],
        compiler_params=pltpu.CompilerParams(vmem_limit_bytes=56 << 20),
        name="serve",
    )(doc_length, arrived, qw, kw, vw)


def gather_sum_kernel(server_ref, back_ref, out_ref):
    total = back_ref[0].astype(jnp.float32)
    for part in range(1, back_ref.shape[0]):
        total = total + back_ref[part].astype(jnp.float32)
    out_ref[...] = total


def gather_sum(unit_server, back):
    _, parts, unit_rows, width = back.shape
    units = unit_server.shape[0]
    return pl.pallas_call(
        gather_sum_kernel,
        out_shape=jax.ShapeDtypeStruct((units * unit_rows, width), jnp.float32),
        grid_spec=pltpu.PrefetchScalarGridSpec(
            num_scalar_prefetch=1,
            grid=(units,),
            in_specs=[
                pl.BlockSpec(
                    (pl.Squeezed(), parts, unit_rows, width), lambda u, server: (server[u], 0, 0, 0)
                )
            ],
            out_specs=pl.BlockSpec((unit_rows, width), lambda u, server: (u, 0)),
        ),
        name="gather_sum",
    )(unit_server, back)


def local(
    saved_query,
    saved_key,
    saved_value,
    grad_output,
    unit_server,
    unit_place,
    doc_length,
    query_weight,
    key_weight,
    value_weight,
):
    servers = lax.axis_size("dp")
    parts = lax.axis_size("mp")
    doc_count = doc_length.shape[0]
    outgoing = pack(unit_server, unit_place, saved_query, saved_key, saved_value, grad_output)
    arrived = lax.all_to_all(outgoing, "dp", split_axis=0, concat_axis=0, tiled=True)
    slots, unit_rows, _ = arrived.shape
    order = None
    if doc_count > 1:
        place = arrived[:, 0, -1].astype(jnp.int32)
        order = jnp.argsort(place)
        arrived = arrived[order]
    partial = serve(doc_length, arrived, query_weight, key_weight, value_weight, parts)
    if order is not None:
        partial = partial[place]
    width = partial.shape[-1]
    back = lax.all_to_all(
        partial.reshape(slots * parts, unit_rows, width),
        ("dp", "mp"),
        split_axis=0,
        concat_axis=0,
        tiled=True,
    )
    return gather_sum(unit_server, back.reshape(servers, parts, unit_rows, width))


def solution(mesh):
    placed = (
        P("dp", "mp"),
        P("dp", "mp"),
        P("dp", "mp"),
        P("dp", "mp"),
        P("dp"),
        P("dp"),
        P("dp"),
        P(None, "mp"),
        P(None, "mp"),
        P(None, "mp"),
    )
    return jax.shard_map(
        local, mesh=mesh, in_specs=placed, out_specs=P("dp", "mp"), check_vma=False
    )
```

time: 193 us -> 97.6 us (0.51)
  waiting for transfers between devices: 106 us -> 18.2 us
  blocking collectives: 0 us -> 51.5 us
  local copies, waits for them, and re-layouts: 31.6 us -> 1.08 us
  Pallas kernels: 0 us -> 19.4 us
  starting transfers between devices: 22.6 us -> 5.2 us
  matrix products: 13.7 us -> 0 us
  between operations: 14.3 us -> 0.66 us
  other arithmetic: 3.74 us -> 0 us
    reduce_scatter x1 -> x0, waiting for transfers between devices: 76.3 us -> none  [local(): lax.psum_scatter(partial_value, 'mp', scatter_dimension=1, tiled=True)]
    all_to_all x0 -> x1, blocking collectives: none -> 51.5 us  [local(): lax.all_to_all(partial.reshape(slots * parts, unit_rows, width), ('dp', '...]
    pallas_call x0 -> x3, Pallas kernels: none -> 19.4 us  [the longest x1 10.7 us: serve(): pl.pallas_call(functools.partial(server_kernel, kv_heads, min(256, part_w...]
    all_to_all x6 -> x1, starting transfers between devices: 22.6 us -> 5.2 us  [local(): lax.all_to_all(outgoing, 'dp', split_axis=0, concat_axis=0, tiled=True)]
    scatter x6 -> x0, local copies, waits for them, and re-layouts: 13.4 us -> none  [the longest x4 9.46 us: outgoing(): return jnp.zeros((server_count, unit_rows, tensor.shape[1]), tensor.dtype...]
    dot_general x8 -> x0, matrix products: 11.4 us -> none  [the longest x1 5.77 us: project(): lax.dot_general(grads[0], query_weight, numbers, preferred_element_type=j...]
    all_to_all x6 -> x1, waiting for transfers between devices: 29.5 us -> 18.2 us  [local(): lax.all_to_all(outgoing, 'dp', split_axis=0, concat_axis=0, tiled=True)]
    another operation x12 -> x0, local copies, waits for them, and re-layouts: 9.4 us -> none  [the longest x2 3.56 us: tile_backward(): queries = query_rows.reshape(query_count, kv_heads, group_size, HEAD)]
  transfers between devices with their start and end apart: 7 -> 1, of which waited for: 7 -> 1; matrix products, arithmetic and copies ran while one was open for 10% -> 0% of each run, Pallas kernels for 0% -> 0%
where the time goes in v1:
time: 97.6 us; the launch traced here: 96.1 us
  blocking collectives  51.5 us (53%)
  Pallas kernels  19.4 us (20%)
  waiting for transfers between devices  18.2 us (19%)
  starting transfers between devices  5.2 us (5%)
  local copies, waits for them, and re-layouts  1.08 us (1%)
    all_to_all x1, blocking collectives, local(): lax.all_to_all(partial.reshape(slots * parts, unit_rows, width), ('dp', '...  51.5 us
    all_to_all x1, waiting for transfers between devices, local(): lax.all_to_all(outgoing, 'dp', split_axis=0, concat_axis=0, tiled=True)  18.2 us
    pallas_call x1, Pallas kernels, serve(): pl.pallas_call(functools.partial(server_kernel, kv_heads, min(256, part_w...  10.7 us
    pallas_call x1, Pallas kernels, gather_sum(): pl.pallas_call(gather_sum_kernel, out_shape=jax.ShapeDtypeStruct((units *...  6.14 us
    all_to_all x1, starting transfers between devices, local(): lax.all_to_all(outgoing, 'dp', split_axis=0, concat_axis=0, tiled=True)  5.2 us
    pallas_call x1, Pallas kernels, pack(): pl.pallas_call(pack_kernel, out_shape=jax.ShapeDtypeStruct((units, q.shap...  2.52 us
  transfers between devices with their start and end apart: 1, of which 1 were waited for; matrix products, arithmetic and copies ran while one was open for 0% of the time, Pallas kernels for 0%

profile of v1, /device:TPU:0, one launch (start us, length us, event | category | flops | bytes accessed | tf_op | source)
XLA Modules:
  0.0 96.1 jit_solution(15636917216406419145)
XLA Ops:
  0.0 2.5 %pack.1 = bf16[8,32,2688]{2,1,0:T(8,128)(2,1)} custom-call(s32[8]{0:T(128)} %server_ref.3, s32[8]{0:T(128)} %place_ref.1, bf16[256,1024]{1,0:T(8,128)(2,1)} %q_ref.1, bf16[256,256]{1,0:T(8,128)(2,1)} %k_ref.1, bf16[256,256]{1,0:T(8,128)(2,1)} %v_ref.1, bf16[256,1024]{1,0:T(8,128)(2,1)} %g_ref.1), custom_call_target="tpu_custom_call" | custom-call | tf_op jit(solution)/shard_map/pack/pallas_call | solution.py:36
  2.5 5.2 %all-to-all-start = ((bf16[8,32,2688]{2,1,0:T(8,128)(2,1)}), bf16[8,32,2688]{2,1,0:T(8,128)(2,1)S(1)}, u32[]{:S(2)}, u32[]{:S(2)}) async-start(bf16[8,32,2688]{2,1,0:T(8,128)(2,1)} %pack.1), calls=%async_computation | async-start | bytes 2752512 | tf_op jit(solution)/shard_map/all_to_all | solution.py:236
  8.4 18.2 %all-to-all-done.arrived_ref = bf16[8,32,2688]{2,1,0:T(8,128)(2,1)S(1)} async-done(((bf16[8,32,2688]{2,1,0:T(8,128)(2,1)}), bf16[8,32,2688]{2,1,0:T(8,128)(2,1)S(1)}, u32[]{:S(2)}, u32[]{:S(2)}) %all-to-all-start) | async-done | bytes 1376288 | tf_op jit(solution)/shard_map/all_to_all | solution.py:236
  26.6 0.0 copy-start
  26.6 1.1 %copy-done = bf16[8,32,2688]{2,1,0:T(8,128)(2,1)} copy-done((bf16[8,32,2688]{2,1,0:T(8,128)(2,1)}, bf16[8,32,2688]{2,1,0:T(8,128)(2,1)S(1)}, u32[]{:S(2)}) %copy-start) | copy-done | bytes 1376280
  27.7 10.7 %serve.1 = bf16[8,4,32,1024]{3,2,1,0:T(8,128)(2,1)} custom-call(s32[1]{0:T(128)S(6)} %copy.11.length_ref, bf16[8,32,2688]{2,1,0:T(8,128)(2,1)} %copy-done, bf16[4096,1024]{1,0:T(8,128)(2,1)} %qw_hbm.1, bf16[4096,256]{1,0:T(8,128)(2,1)} %kw_hbm.1, bf16[4096,256]{1,0:T(8,128)(2,1)} %vw_hbm.1), custom_call_target="tpu_custom_call" | custom-call | tf_op jit(solution)/shard_map/serve/pallas_call | solution.py:168
  38.4 51.5 %all_to_all.10 = bf16[32,32,1024]{2,1,0:T(8,128)(2,1)} all-to-all(bf16[32,32,1024]{2,1,0:T(8,128)(2,1)} %bitcast.2), channel_id=1, replica_groups=mesh['dp'=8,'mp'=4] {'dp','mp'}, dimensions={0} | all-to-all | bytes 4194304 | tf_op jit(solution)/shard_map/all_to_all | solution.py:247
  89.9 6.1 %gather_sum.1 = f32[256,1024]{1,0:T(8,128)} custom-call(s32[8]{0:T(128)} %server_ref.3, bf16[8,4,32,1024]{3,2,1,0:T(8,128)(2,1)} %bitcast.3), custom_call_target="tpu_custom_call" | custom-call | tf_op jit(solution)/shard_map/gather_sum/pallas_call | solution.py:203
Async XLA Ops:
  2.5 24.1 %all-to-all-start = ((bf16[8,32,2688]{2,1,0:T(8,128)(2,1)}), bf16[8,32,2688]{2,1,0:T(8,128)(2,1)S(1)}, u32[]{:S(2)}, u32[]{:S(2)}) async-start(bf16[8,32,2688]{2,1,0:T(8,128)(2,1)} %pack.1), calls=%async_computation | async-start | bytes 2752512 | tf_op jit(solution)/shard_map/all_to_all | solution.py:236
  26.6 1.1 %copy-start = (bf16[8,32,2688]{2,1,0:T(8,128)(2,1)}, bf16[8,32,2688]{2,1,0:T(8,128)(2,1)S(1)}, u32[]{:S(2)}) copy-start(bf16[8,32,2688]{2,1,0:T(8,128)(2,1)S(1)} %all-to-all-done.arrived_ref) | copy-start | bytes 4128772

commit v2 on v1

--- a/solution.py
+++ b/solution.py
@@ -11,6 +11,10 @@
 HEAD = 128
 DOC_UNITS = 8
 LANES = 128
+TILE = 128
+PACK_VMEM = 32 << 20
+SERVE_VMEM = 50 << 20
+SUM_VMEM = 12 << 20
 
 
 def pack_kernel(server_ref, place_ref, q_ref, k_ref, v_ref, g_ref, out_ref):
@@ -38,10 +42,12 @@
         out_shape=jax.ShapeDtypeStruct((units, q.shape[0] // units, width), q.dtype),
         in_specs=[smem, smem, vmem, vmem, vmem, vmem],
         out_specs=vmem,
+        compiler_params=pltpu.CompilerParams(vmem_limit_bytes=PACK_VMEM),
         name="pack",
     )(unit_server, unit_place, q, k, v, g)
 
 
+NN = (((1,), (0,)), ((), ()))
 NT = (((1,), (1,)), ((), ()))
 TN = (((0,), (0,)), ((), ()))
 
@@ -58,21 +64,24 @@
     qw_hbm,
     kw_hbm,
     vw_hbm,
-    out_hbm,
+    out_ref,
     qw,
     kw,
     vw,
     grads,
-    partial,
+    bias,
+    queries,
+    masked,
+    probs_low,
+    score_low,
     in_sems,
-    out_sems,
 ):
     doc_count = length_ref.shape[0]
     slots, unit_rows, _ = arrived_ref.shape
     block_rows = slots * unit_rows // doc_count
     doc_slots = slots // doc_count
-    parts = out_hbm.shape[1]
-    part_width = out_hbm.shape[3]
+    parts = out_ref.shape[1]
+    part_width = out_ref.shape[3]
     q_width = qw.shape[1]
     kv_width = kw.shape[1]
     group = q_width // kv_width
@@ -103,43 +112,45 @@
         slot = jnp.floor(row * (1.0 / unit_rows))
         place = place - DOC_UNITS * jnp.floor(place * (1.0 / DOC_UNITS))
         position = place * unit_rows + (row - slot * unit_rows)
-        query_at = position[:, :1]
-        key_at = jnp.transpose(position)[:1, :]
+        live = position < length
+        key_at = position[:, :1]
+        query_at = jnp.transpose(position)[:1, :]
         allowed = (key_at <= query_at) & (key_at < length)
-        live = query_at < length
+        bias[...] = jnp.where(allowed, 0.0, -1e30)
+        tiles = block_rows // TILE
         for kv in range(kv_heads):
             keys = load(q_width + kv * HEAD, HEAD)
             values = load(q_width + kv_width + kv * HEAD, HEAD)
-            key_grad = None
-            value_grad = None
-            for h in range(kv * group, (kv + 1) * group):
-                queries = load(h * HEAD, HEAD)
-                outer = load(q_width + 2 * kv_width + h * HEAD, HEAD)
-                masked = jnp.where(live, outer.astype(jnp.float32), 0.0).astype(jnp.bfloat16)
-                scores = dot(queries, keys, NT) * scale
-                scores = jnp.where(allowed, scores, -1e30)
-                peak = jnp.max(scores, axis=1, keepdims=True)
-                expanded = jnp.where(allowed, jnp.exp(scores - peak), 0.0)
-                probs = expanded * (1.0 / jnp.sum(expanded, axis=1, keepdims=True))
-                probs_low = probs.astype(jnp.bfloat16)
-                prob_grad = dot(masked, values, NT)
-                delta = jnp.sum(probs_low.astype(jnp.float32) * prob_grad, axis=1, keepdims=True)
-                score_low = (probs * (prob_grad - delta)).astype(jnp.bfloat16)
-                query_grad = dot(score_low, keys, (((1,), (0,)), ((), ()))) * scale
-                grads[rows, h * HEAD : (h + 1) * HEAD] = query_grad.astype(jnp.bfloat16)
-                dk = dot(score_low, queries, TN)
-                dv = dot(probs_low, masked, TN)
-                key_grad = dk if key_grad is None else key_grad + dk
-                value_grad = dv if value_grad is None else value_grad + dv
+            for h in range(group):
+                head = kv * group + h
+                here_rows = slice(h * block_rows, (h + 1) * block_rows)
+                queries[here_rows, :] = load(head * HEAD, HEAD)
+                outer = load(q_width + 2 * kv_width + head * HEAD, HEAD).astype(jnp.float32)
+                masked[here_rows, :] = jnp.where(live, outer, 0.0).astype(jnp.bfloat16)
+            for t in range(group * tiles):
+                at = t * TILE
+                within = (t % tiles) * TILE
+                scores = dot(keys, queries[at : at + TILE, :], NT) * scale
+                scores = scores + bias[:, within : within + TILE]
+                peak = jnp.max(scores, axis=0, keepdims=True)
+                expanded = jnp.exp(scores - peak)
+                probs = expanded * (1.0 / jnp.sum(expanded, axis=0, keepdims=True))
+                low = probs.astype(jnp.bfloat16)
+                probs_low[:, at : at + TILE] = low
+                prob_grad = dot(values, masked[at : at + TILE, :], NT)
+                delta = jnp.sum(low.astype(jnp.float32) * prob_grad, axis=0, keepdims=True)
+                score_low[:, at : at + TILE] = (probs * (prob_grad - delta)).astype(jnp.bfloat16)
             at = q_width + kv * HEAD
-            grads[rows, at : at + HEAD] = (key_grad * scale).astype(jnp.bfloat16)
+            grads[rows, at : at + HEAD] = (
+                dot(score_low[...], queries[...], NN) * scale
+            ).astype(jnp.bfloat16)
             at = q_width + kv_width + kv * HEAD
-            grads[rows, at : at + HEAD] = value_grad.astype(jnp.bfloat16)
-
-    def out_copy(part):
-        return pltpu.make_async_copy(
-            partial.at[part], out_hbm.at[:, part], out_sems.at[part]
-        )
+            grads[rows, at : at + HEAD] = dot(probs_low[...], masked[...], NN).astype(jnp.bfloat16)
+            for h in range(group):
+                at = (kv * group + h) * HEAD
+                grads[rows, at : at + HEAD] = (
+                    dot(score_low[:, h * block_rows : (h + 1) * block_rows], keys, TN) * scale
+                ).astype(jnp.bfloat16)
 
     for part in range(parts):
         for copy in weight_copies(part):
@@ -149,12 +160,9 @@
             total = dot(grads[:, :q_width], qw[columns, :], NT)
             total = total + dot(grads[:, q_width : q_width + kv_width], kw[columns, :], NT)
             total = total + dot(grads[:, q_width + kv_width :], vw[columns, :], NT)
-            partial[part, :, :, at : at + tile] = total.astype(jnp.bfloat16).reshape(
+            out_ref[:, part, :, at : at + tile] = total.astype(jnp.bfloat16).reshape(
                 slots, unit_rows, tile
             )
-        out_copy(part).start()
-    for part in range(parts):
-        out_copy(part).wait()
 
 
 def serve(doc_length, arrived, qw, kw, vw, parts):
@@ -163,7 +171,9 @@
     part_width = width // parts
     kv_heads = kw.shape[1] // HEAD
     rows = slots * unit_rows
-    hbm = pl.BlockSpec(memory_space=pl.ANY)
+    block = rows // doc_length.shape[0]
+    group = qw.shape[1] // kw.shape[1]
+    hbm = pl.BlockSpec(memory_space=pltpu.HBM)
     bf16 = jnp.bfloat16
     return pl.pallas_call(
         functools.partial(server_kernel, kv_heads, min(256, part_width)),
@@ -175,44 +185,59 @@
             hbm,
             hbm,
         ],
-        out_specs=hbm,
+        out_specs=pl.BlockSpec(memory_space=pltpu.VMEM),
         scratch_shapes=[
             pltpu.VMEM(qw.shape, bf16),
             pltpu.VMEM(kw.shape, bf16),
             pltpu.VMEM(vw.shape, bf16),
             pltpu.VMEM((rows, qw.shape[1] + 2 * kw.shape[1]), bf16),
-            pltpu.VMEM((parts, slots, unit_rows, part_width), bf16),
+            pltpu.VMEM((block, block), jnp.float32),
+            pltpu.VMEM((group * block, HEAD), bf16),
+            pltpu.VMEM((group * block, HEAD), bf16),
+            pltpu.VMEM((block, group * block), bf16),
+            pltpu.VMEM((block, group * block), bf16),
             pltpu.SemaphoreType.DMA((parts, 3)),
-            pltpu.SemaphoreType.DMA((parts,)),
-        ],
-        compiler_params=pltpu.CompilerParams(vmem_limit_bytes=56 << 20),
+        ],
+        compiler_params=pltpu.CompilerParams(vmem_limit_bytes=SERVE_VMEM),
         name="serve",
     )(doc_length, arrived, qw, kw, vw)
 
 
-def gather_sum_kernel(server_ref, back_ref, out_ref):
-    total = back_ref[0].astype(jnp.float32)
-    for part in range(1, back_ref.shape[0]):
-        total = total + back_ref[part].astype(jnp.float32)
-    out_ref[...] = total
+def gather_sum_kernel(server_ref, back_ref, out_hbm, total, sems):
+    units, unit_rows, _ = total.shape
+
+    def out_copy(u):
+        return pltpu.make_async_copy(
+            total.at[u], out_hbm.at[pl.ds(u * unit_rows, unit_rows)], sems.at[u]
+        )
+
+    for u in range(units):
+        server = server_ref[u]
+        summed = back_ref[server, 0].astype(jnp.float32)
+        for part in range(1, back_ref.shape[1]):
+            summed = summed + back_ref[server, part].astype(jnp.float32)
+        total[u] = summed
+        out_copy(u).start()
+    for u in range(units):
+        out_copy(u).wait()
 
 
 def gather_sum(unit_server, back):
-    _, parts, unit_rows, width = back.shape
+    _, _, unit_rows, width = back.shape
     units = unit_server.shape[0]
     return pl.pallas_call(
         gather_sum_kernel,
         out_shape=jax.ShapeDtypeStruct((units * unit_rows, width), jnp.float32),
-        grid_spec=pltpu.PrefetchScalarGridSpec(
-            num_scalar_prefetch=1,
-            grid=(units,),
-            in_specs=[
-                pl.BlockSpec(
-                    (pl.Squeezed(), parts, unit_rows, width), lambda u, server: (server[u], 0, 0, 0)
-                )
-            ],
-            out_specs=pl.BlockSpec((unit_rows, width), lambda u, server: (u, 0)),
-        ),
+        in_specs=[
+            pl.BlockSpec(memory_space=pltpu.SMEM),
+            pl.BlockSpec(memory_space=pltpu.VMEM),
+        ],
+        out_specs=pl.BlockSpec(memory_space=pl.ANY),
+        scratch_shapes=[
+            pltpu.VMEM((units, unit_rows, width), jnp.float32),
+            pltpu.SemaphoreType.DMA((units,)),
+        ],
+        compiler_params=pltpu.CompilerParams(vmem_limit_bytes=SUM_VMEM),
         name="gather_sum",
     )(unit_server, back)
 

time: 97.6 us -> 94 us (0.963)
  Pallas kernels: 19.4 us -> 11.9 us
  local copies, waits for them, and re-layouts: 1.08 us -> 5.21 us
    pallas_call x1, Pallas kernels: 6.14 us -> 1.6 us  [gather_sum(): pl.pallas_call(gather_sum_kernel, out_shape=jax.ShapeDtypeStruct((units *...]
    unnamed x2 -> x14, local copies, waits for them, and re-layouts: 1.08 us -> 5.21 us
    pallas_call x1, Pallas kernels: 10.7 us -> 8.58 us  [serve(): pl.pallas_call(functools.partial(server_kernel, kv_heads, min(256, part_w...]
where the time goes in v2:
time: 94 us; the launch traced here: 92.5 us
  blocking collectives  51.2 us (54%)
  waiting for transfers between devices  18.2 us (19%)
  Pallas kernels  11.9 us (13%)
  local copies, waits for them, and re-layouts  5.21 us (6%)
  starting transfers between devices  5.2 us (6%)
    all_to_all x1, blocking collectives, local(): lax.all_to_all(partial.reshape(slots * parts, unit_rows, width), ('dp', '...  51.2 us
    all_to_all x1, waiting for transfers between devices, local(): lax.all_to_all(outgoing, 'dp', split_axis=0, concat_axis=0, tiled=True)  18.2 us
    pallas_call x1, Pallas kernels, serve(): pl.pallas_call(functools.partial(server_kernel, kv_heads, min(256, part_w...  8.58 us
    unnamed x14, local copies, waits for them, and re-layouts  5.21 us
    all_to_all x1, starting transfers between devices, local(): lax.all_to_all(outgoing, 'dp', split_axis=0, concat_axis=0, tiled=True)  5.2 us
  transfers between devices with their start and end apart: 1, of which 1 were waited for; matrix products, arithmetic and copies ran while one was open for 0% of the time, Pallas kernels for 0%

profile of v2, /device:TPU:0, one launch (start us, length us, event | category | flops | bytes accessed | tf_op | source)
XLA Modules:
  0.0 92.5 jit_solution(10316298982231026416)
XLA Ops:
  0.0 0.0 copy-start
  0.0 1.0 %copy-done = bf16[256,1024]{1,0:T(8,128)(2,1)S(1)} copy-done((bf16[256,1024]{1,0:T(8,128)(2,1)S(1)}, bf16[256,1024]{1,0:T(8,128)(2,1)}, u32[]{:S(2)}) %copy-start) | copy-done | bytes 524312
  1.0 0.0 copy-start.1
  1.0 1.0 %copy-done.1 = bf16[256,1024]{1,0:T(8,128)(2,1)S(1)} copy-done((bf16[256,1024]{1,0:T(8,128)(2,1)S(1)}, bf16[256,1024]{1,0:T(8,128)(2,1)}, u32[]{:S(2)}) %copy-start.1) | copy-done | bytes 524312
  2.1 0.0 copy-start.2
  2.1 0.9 copy-done.2
  3.0 0.0 copy-start.3
  3.0 0.9 copy-done.3
  3.9 0.0 copy-start.4
  3.9 0.7 copy-done.4
  4.5 0.0 copy-start.6
  4.6 0.7 copy-done.6
  5.2 1.7 %pack.1 = bf16[8,32,2688]{2,1,0:T(8,128)(2,1)} custom-call(s32[8]{0:T(128)S(1)} %copy-done.4, s32[8]{0:T(128)S(1)} %copy-done.6, bf16[256,1024]{1,0:T(8,128)(2,1)S(1)} %copy-done, bf16[256,256]{1,0:T(8,128)(2,1)S(1)} %copy-done.2, bf16[256,256]{1,0:T(8,128)(2,1)S(1)} %copy-done.3, bf16[256,1024]{1,0:T(8,128)(2,1)S(1)} %copy-done.1), custom_call_target="tpu_custom_call" | custom-call | tf_op jit(solution)/shard_map/pack/pallas_call | solution.py:40
  7.0 5.2 %all-to-all-start = ((bf16[8,32,2688]{2,1,0:T(8,128)(2,1)}), bf16[8,32,2688]{2,1,0:T(8,128)(2,1)S(1)}, u32[]{:S(2)}, u32[]{:S(2)}) async-start(bf16[8,32,2688]{2,1,0:T(8,128)(2,1)} %pack.1), calls=%async_computation | async-start | bytes 2752512 | tf_op jit(solution)/shard_map/all_to_all | solution.py:261
  12.8 18.2 %all-to-all-done.arrived_ref = bf16[8,32,2688]{2,1,0:T(8,128)(2,1)S(1)} async-done(((bf16[8,32,2688]{2,1,0:T(8,128)(2,1)}), bf16[8,32,2688]{2,1,0:T(8,128)(2,1)S(1)}, u32[]{:S(2)}, u32[]{:S(2)}) %all-to-all-start) | async-done | bytes 1376288 | tf_op jit(solution)/shard_map/all_to_all | solution.py:261
  31.0 8.6 %serve.1 = bf16[8,4,32,1024]{3,2,1,0:T(8,128)(2,1)S(1)} custom-call(s32[1]{0:T(128)S(6)} %copy.11.length_ref, bf16[8,32,2688]{2,1,0:T(8,128)(2,1)S(1)} %all-to-all-done.arrived_ref, bf16[4096,1024]{1,0:T(8,128)(2,1)} %qw_hbm.1, bf16[4096,256]{1,0:T(8,128)(2,1)} %kw_hbm.1, bf16[4096,256]{1,0:T(8,128)(2,1)} %vw_hbm.1), custom_call_target="tpu_custom_call" | custom-call | tf_op jit(solution)/shard_map/serve/pallas_call | solution.py:178
  39.6 0.0 copy-start.5
  39.6 51.2 %all_to_all.10 = bf16[32,32,1024]{2,1,0:T(8,128)(2,1)S(1)} all-to-all(bf16[32,32,1024]{2,1,0:T(8,128)(2,1)S(1)} %bitcast.2), channel_id=1, replica_groups=mesh['dp'=8,'mp'=4] {'dp','mp'}, dimensions={0} | all-to-all | bytes 4194304 | tf_op jit(solution)/shard_map/all_to_all | solution.py:272
  90.9 0.0 copy-done.5
  90.9 1.6 %gather_sum.1 = f32[256,1024]{1,0:T(8,128)} custom-call(s32[8]{0:T(128)S(1)} %copy-done.5, bf16[8,4,32,1024]{3,2,1,0:T(8,128)(2,1)S(1)} %bitcast.3), custom_call_target="tpu_custom_call" | custom-call | tf_op jit(solution)/shard_map/gather_sum/pallas_call | solution.py:228
Async XLA Ops:
  0.0 1.0 %copy-start = (bf16[256,1024]{1,0:T(8,128)(2,1)S(1)}, bf16[256,1024]{1,0:T(8,128)(2,1)}, u32[]{:S(2)}) copy-start(bf16[256,1024]{1,0:T(8,128)(2,1)} %q_ref.1) | copy-start | bytes 1572868
  1.0 1.0 %copy-start.1 = (bf16[256,1024]{1,0:T(8,128)(2,1)S(1)}, bf16[256,1024]{1,0:T(8,128)(2,1)}, u32[]{:S(2)}) copy-start(bf16[256,1024]{1,0:T(8,128)(2,1)} %g_ref.1) | copy-start | bytes 1572868
  2.1 0.9 copy-start.2
  3.0 0.9 copy-start.3
  3.9 0.7 copy-start.4
  4.5 0.7 copy-start.6
  7.0 24.1 %all-to-all-start = ((bf16[8,32,2688]{2,1,0:T(8,128)(2,1)}), bf16[8,32,2688]{2,1,0:T(8,128)(2,1)S(1)}, u32[]{:S(2)}, u32[]{:S(2)}) async-start(bf16[8,32,2688]{2,1,0:T(8,128)(2,1)} %pack.1), calls=%async_computation | async-start | bytes 2752512 | tf_op jit(solution)/shard_map/all_to_all | solution.py:261
  39.6 51.2 %copy-start.5 = (s32[8]{0:T(128)S(1)}, s32[8]{0:T(128)}, u32[]{:S(2)}) copy-start(s32[8]{0:T(128)} %server_ref.3) | copy-start | bytes 100
